TPU v7x, 32 devices: a whole 2x2x4 slice. The times are simulated.
32 devices in a mesh: ctx: 8 (over y, x, core), dp: 4 (over z).
Axes of the slice: x: 2, y: 2, z: 4, core: 2. Of those that a mesh axis runs over, the one named last changes fastest.
Arguments:
- query_previous: bfloat16 [4, 1024, 2048], P('dp', 'ctx'), may hold values from -240 to 240
- key_previous: bfloat16 [4, 1024, 512], P('dp', 'ctx'), may hold values from -6 to 6
- value_previous: bfloat16 [4, 1024, 512], P('dp', 'ctx'), may hold values from -6 to 6
- span_order: int32 [16], replicated, may hold values from 0 to 15, each once
- resid: bfloat16 [4, 1024, 4096], P('dp', 'ctx'), may hold values from -6 to 6
- grad_norm: bfloat16 [4, 1024, 4096], P('dp', 'ctx'), may hold values from -3 to 3
- gain: float32 [4096], replicated, may hold values from 0.1 to 1.9
Outputs:
- out_prev: bfloat16 [4, 1024, 2048], P('dp', 'ctx')
- lse_prev: float32 [4, 16, 1024], P('dp', None, 'ctx')
- resid_grad: bfloat16 [4, 1024, 4096], P('dp', 'ctx')
- gain_grad: float32 [4096], replicated
Inputs may be any that keep to these rules, and one draw needn't show every extreme that they name: span_order names each of the 16 spans once; rows c * 64 to (c + 1) * 64 - 1 of a sequence's arrays hold span span_order[c].
All inputs are finite; a program needn't handle non-finite values.
Results may differ from a plain program's by a relative error of at most 0.0055.
Values may be sent and summed in bfloat16 or wider, within the bound.
No kernel may reach another device: no remote copies, remote signals or barrier semaphores. Data moves between devices by JAX's collectives and lax.ppermute only.
A program may use at most 64 MiB of HBM per device.

v0:
```python
import math
import jax
import jax.numpy as jnp
from jax import lax
from jax.sharding import PartitionSpec as P

QUERY_HEADS = 16
KEY_VALUE_HEADS = 4
HEAD_WIDTH = 128


def key_positions(tally_count, span_order, half):
    index = jnp.arange(tally_count, dtype=jnp.int32)
    slot = index // half
    table = slot[:, None] == jnp.arange(span_order.shape[0], dtype=jnp.int32)[None, :]
    chosen = jnp.sum(jnp.where(table, span_order[None, :], 0), axis=1)
    return chosen * half + index % half


def dense_update(query_rows, q_positions, carry, key_rows, value_rows, k_positions):
    top, total, summed = carry
    scores = jnp.einsum(
        "rkgd,skd->kgrs", query_rows, key_rows, preferred_element_type=jnp.float32
    ) * HEAD_WIDTH ** (-0.5)
    mask = (k_positions[None, :] <= q_positions[:, None])[None, None]
    scores = jnp.where(mask, scores, -1e30)
    new_top = jnp.maximum(top, jnp.max(scores, axis=-1))
    weights = jnp.where(mask, jnp.exp(scores - new_top[..., None]), 0.0)
    factor = jnp.exp(top - new_top)
    total = total * factor + jnp.sum(weights, axis=-1)
    probs = weights.astype(jnp.bfloat16)
    added = jnp.einsum("kgrs,skd->rkgd", probs, value_rows, preferred_element_type=jnp.float32)
    summed = summed * jnp.transpose(factor, (2, 0, 1))[..., None] + added
    return (new_top, total, summed)


def update(query_rows, q_positions, carry, key_rows, value_rows, k_positions):
    later = jnp.min(k_positions) > jnp.max(q_positions)
    return lax.cond(
        later,
        lambda state: state,
        lambda state: dense_update(
            query_rows, q_positions, state, key_rows, value_rows, k_positions
        ),
        carry,
    )


def fold_piece(query_rows, q_positions, carry, k_piece, v_piece, span_order, half):
    tally_count = k_piece.shape[1]
    heads = k_piece.shape[2] // HEAD_WIDTH
    key_rows = k_piece[0].reshape(tally_count, heads, HEAD_WIDTH)
    value_rows = v_piece[0].reshape(tally_count, heads, HEAD_WIDTH)
    k_positions = key_positions(tally_count, span_order, half)
    block = math.gcd(tally_count, 512)
    steps = tally_count // block

    def step_fn(state, items):
        return (update(query_rows, q_positions, state, items[0], items[1], items[2]), None)

    carry, unused = lax.scan(
        step_fn,
        carry,
        (
            key_rows.reshape(steps, block, heads, HEAD_WIDTH),
            value_rows.reshape(steps, block, heads, HEAD_WIDTH),
            k_positions.reshape(steps, block),
        ),
    )
    return carry


def blank_state(heads, query_group, row_indices):
    return (
        jnp.full((heads, query_group, row_indices), -1e30, jnp.float32),
        jnp.zeros((heads, query_group, row_indices), jnp.float32),
        jnp.zeros((row_indices, heads, query_group, HEAD_WIDTH), jnp.float32),
    )


def attention(query_previous, key_previous, value_previous, span_order):
    row_indices = query_previous.shape[1]
    half = row_indices // 2
    query_group = QUERY_HEADS // KEY_VALUE_HEADS
    mine = lax.dynamic_slice_in_dim(span_order, 2 * lax.axis_index("ctx"), 2)
    local = jnp.arange(row_indices, dtype=jnp.int32)
    q_positions = jnp.where(local < half, mine[0], mine[1]) * half + local % half
    query_rows = query_previous[0].reshape(row_indices, KEY_VALUE_HEADS, query_group, HEAD_WIDTH)
    top, total, summed = fold_piece(
        query_rows,
        q_positions,
        blank_state(KEY_VALUE_HEADS, query_group, row_indices),
        lax.all_gather(key_previous, "ctx", axis=1, tiled=True),
        lax.all_gather(value_previous, "ctx", axis=1, tiled=True),
        span_order,
        half,
    )
    output = summed / jnp.transpose(total, (2, 0, 1))[..., None]
    out_prev = output.reshape(1, row_indices, QUERY_HEADS * HEAD_WIDTH).astype(jnp.bfloat16)
    lse_prev = (top + jnp.log(total)).reshape(1, QUERY_HEADS, row_indices)
    return (out_prev, lse_prev)


def norm_backward(resid, grad_norm, gain):
    resid_f = resid[0].astype(jnp.float32)
    grad_f = grad_norm[0].astype(jnp.float32)
    inv_rms = 1.0 / jnp.sqrt(jnp.mean(resid_f * resid_f, axis=-1, keepdims=True) + 1e-05)
    normed = resid_f * inv_rms
    partial_grad = jnp.sum(grad_f * normed, axis=0)
    gain_grad = lax.psum(partial_grad, ("ctx", "dp"))
    scaled = gain[None, :] * grad_f
    resid_grad = (
        (scaled - normed * jnp.mean(scaled * normed, axis=-1, keepdims=True)) * inv_rms
    ).astype(jnp.bfloat16)
    return (gain_grad, resid_grad[None])


def per_device(query_previous, key_previous, value_previous, span_order, resid, grad_norm, gain):
    out_prev, lse_prev = attention(query_previous, key_previous, value_previous, span_order)
    gain_grad, resid_grad = norm_backward(resid, grad_norm, gain)
    return (out_prev, lse_prev, resid_grad, gain_grad)


def solution(mesh):
    return jax.shard_map(
        per_device,
        mesh=mesh,
        in_specs=(
            P("dp", "ctx", None),
            P("dp", "ctx", None),
            P("dp", "ctx", None),
            P(),
            P("dp", "ctx", None),
            P("dp", "ctx", None),
            P(),
        ),
        out_specs=(P("dp", "ctx", None), P("dp", None, "ctx"), P("dp", "ctx", None), P()),
        check_vma=False,
    )
```

profile of v0, /device:TPU:1, one launch (start us, length us, event | category | flops | bytes accessed | tf_op | source)
XLA Modules:
  0.0 89.6 jit_solution(13001923617092184318)
XLA Ops:
  8.7 0.7 dynamic_slice.27
  10.0 1.3 %copy.20 = bf16[1,128,2048]{1,2,0:T(8,128)(2,1)S(1)} copy(bf16[1,128,2048]{2,1,0:T(8,128)(2,1)} %param.11) | data formatting | bytes 1048576 | tf_op args[0]
  11.6 0.7 select_reduce_fusion
  12.4 1.5 %fusion.38 = f32[128]{0:T(128)S(1)} fusion(bf16[1,128,4096]{2,1,0:T(8,128)(2,1)} %param.15), kind=kLoop, calls=%fused_computation.45 | loop fusion | flops 1572736 | bytes 1049088 | tf_op jit(solution)/shard_map/reduce_sum | solution.py:107
  13.9 1.9 %fusion.47 = s32[]{:T(128)} fusion(s32[]{:T(128)} %bitcast.11, s32[]{:T(128)} %bitcast.10), kind=kLoop, calls=%fused_computation.69 | loop fusion | flops 1407 | bytes 12 | tf_op jit(solution)/shard_map/while/body/eval_jaxpr/reduce_max | solution.py:38
  15.9 2.4 %fusion.34 = (f32[4096]{0:T(1024)S(1)}, f32[128]{0:T(128)S(1)}) fusion(bf16[1,128,4096]{2,1,0:T(8,128)(2,1)} %param.15, bf16[1,128,4096]{2,1,0:T(8,128)(2,1)} %param.16, f32[128]{0:T(128)S(1)} %add_rsqrt_fusion, f32[4096]{0:T(1024)} %param.17), kind=kLoop, calls=%fused_computation.41 | loop fusion | flops 4190080 | bytes 2130944 | tf_op jit(solution)/shard_map/reduce_sum | solution.py:109
  18.2 42.3 %psum.7 = f32[4096]{0:T(1024)} all-reduce(f32[4096]{0:T(1024)S(1)} %get-tuple-element.291), channel_id=1, replica_groups=mesh['ctx'=8,'dp'=4] {'ctx','dp'}, use_global_device_ids=true, to_apply=%region_12.13 | all-reduce | flops 4096 | bytes 32768 | tf_op jit(solution)/shard_map/psum | solution.py:110
  60.5 1.5 %fusion.37 = bf16[1,128,4096]{2,1,0:T(8,128)(2,1)} fusion(bf16[1,128,4096]{2,1,0:T(8,128)(2,1)S(1)} %copy-done.1, bf16[1,128,4096]{2,1,0:T(8,128)(2,1)S(1)} %copy-done, f32[128]{0:T(128)S(1)} %broadcast_multiply_fusion.1, f32[128]{0:T(128)S(1)} %add_rsqrt_fusion, f32[4096]{0:T(1024)S(1)} %copy-done.3), kind=kLoop, calls=%fused_computation.44 | loop fusion | flops 4194304 | bytes 3163136 | tf_op jit(solution)/shard_map/convert_element_type | solution.py:114
  62.1 1.3 %reshape_reshape_squeeze.6 = bf16[2,512,4,128]{3,2,1,0:T(4,128)(2,1)S(1)} reshape(bf16[1,1024,512]{2,1,0:T(8,128)(2,1)} %all-gather.3.cloned.1.call-done) | data formatting | bytes 2097152 | tf_op jit(solution)/shard_map/reshape;reshape;squeeze | solution.py:65
  63.6 1.3 %reshape_reshape_squeeze.7 = bf16[2,512,4,128]{3,2,1,0:T(4,128)(2,1)S(1)} reshape(bf16[1,1024,512]{2,1,0:T(8,128)(2,1)} %all-gather.5.cloned.1.call-done) | data formatting | bytes 2097152 | tf_op jit(solution)/shard_map/reshape;reshape;squeeze | solution.py:66
  64.9 1.1 %copy.23 = bf16[2,512,4,128]{3,1,2,0:T(8,128)(2,1)} copy(bf16[2,512,4,128]{3,2,1,0:T(4,128)(2,1)S(1)} %reshape_reshape_squeeze.7) | data formatting | bytes 2097152
  66.2 14.0 %while.16 = (s32[]{:T(128)}, f32[4,4,128]{2,1,0:T(4,128)S(1)}, f32[4,4,128]{2,1,0:T(4,128)S(1)}, f32[128,4,4,128]{3,0,2,1:T(8,128)S(1)}, s32[2,512]{1,0:T(2,128)...) while((s32[]{:T(128)}, f32[4,4,128]{2,1,0:T(4,128)S(1)}, ...), condition=%wide.region_8.9_spmd.clone, body=%wide.region_2.8_spmd.clone.sunk | while | flops 551100160 | bytes 20852624 | solution.py:61
  66.2 0.7 fusion.52
  68.2 5.0 %conditional.3 = ((f32[4,4,128]{2,1,0:T(4,128)S(1)}, f32[4,4,128]{2,1,0:T(4,128)S(1)}, f32[128,4,4,128]{3,0,2,1:T(8,128)S(1)})) conditional(s32[]{:T(128)} %convert_element_type.103, (s32[1,512]{1,0:T(1,128)S(1)}, s32[128]{0:T(128)S(1)}, bf16[2,512,4,128]{3,1,2,0:T(8,128)(2,1)S(1)}, s32[]{:T(128)}, bf16[128,4,4,128]{3,0,2,1:T(8,128)(2,1)S(1)}, ...), branch_computations={%region_4.6_spmd.clone, %region_7.7_spmd} | conditional | flops 551099520 | bytes 20846672 | solution.py:39
  68.2 1.3 %fusion.24 = s32[128]{0:T(128)S(1)} fusion(s32[128]{0:T(128)S(1)} %get-tuple-element.268, s32[128]{0:T(128)S(1)} %get-tuple-element.267, s32[128]{0:T(128)S(1)} %get-tuple-element.272, s32[128]{0:T(128)S(1)} %get-tuple-element.272, s32[128]{0:T(128)S(1)} %get-tuple-element.272, s32[128]{0:T(128)S(1)} %get-tuple-element.272, s32[]{:T(128)} %get-tuple-element.273, ...), kind=kLoop, calls=%fused_computation.25 | loop fusion | flops 1152 | bytes 3596 | tf_op jit(solution)/shard_map/add | solution.py:87
  69.7 0.8 fusion.2
  70.4 1.0 %fusion.4 = f32[4,4,128]{2,1,0:T(4,128)S(1)} fusion(f32[4,512,128,4]{2,1,3,0:T(8,128)S(1)} %get-tuple-element.320, f32[4,4,128]{2,1,0:T(4,128)S(1)} %get-tuple-element.400, pred[128,512]{0,1:T(8,128)(4,1)S(1)} %broadcast_compare_fusion), kind=kLoop, calls=%fused_computation.5 | loop fusion | flops 5240832 | bytes 4276224 | tf_op jit(solution)/shard_map/while/body/eval_jaxpr/cond/branch_0_fun/reduce_sum | solution.py:30
  71.5 1.7 %fusion.11 = f32[128,4,4,128]{3,0,2,1:T(8,128)S(1)} fusion(f32[4,512,128,4]{2,1,3,0:T(8,128)S(1)} %get-tuple-element.320, f32[4,4,128]{2,1,0:T(4,128)S(1)} %get-tuple-element.400, pred[128,512]{0,1:T(8,128)(4,1)S(1)} %broadcast_compare_fusion, f32[128,4,4,128]{3,0,2,1:T(8,128)S(1)} %get-tuple-element.261, bf16[2,512,4,128]{3,1,2,0:T(8,128)(2,1)S(1)} %copy-done.2, ...), kind=kOutput, calls=%fused_computation.9 | convolution fusion | flops 274202624 | bytes 6897668 | tf_op jit(solution)/shard_map/while/body/eval_jaxpr/cond/branch_0_fun/kgrs,skd->rkgd/dot_general | solution.py:32
  75.2 5.0 %conditional.3 = ((f32[4,4,128]{2,1,0:T(4,128)S(1)}, f32[4,4,128]{2,1,0:T(4,128)S(1)}, f32[128,4,4,128]{3,0,2,1:T(8,128)S(1)})) conditional(s32[]{:T(128)} %convert_element_type.103, (s32[1,512]{1,0:T(1,128)S(1)}, s32[128]{0:T(128)S(1)}, bf16[2,512,4,128]{3,1,2,0:T(8,128)(2,1)S(1)}, s32[]{:T(128)}, bf16[128,4,4,128]{3,0,2,1:T(8,128)(2,1)S(1)}, ...), branch_computations={%region_4.6_spmd.clone, %region_7.7_spmd} | conditional | flops 551099520 | bytes 20846672 | solution.py:39
  75.3 1.3 %fusion.24 = s32[128]{0:T(128)S(1)} fusion(s32[128]{0:T(128)S(1)} %get-tuple-element.268, s32[128]{0:T(128)S(1)} %get-tuple-element.267, s32[128]{0:T(128)S(1)} %get-tuple-element.272, s32[128]{0:T(128)S(1)} %get-tuple-element.272, s32[128]{0:T(128)S(1)} %get-tuple-element.272, s32[128]{0:T(128)S(1)} %get-tuple-element.272, s32[]{:T(128)} %get-tuple-element.273, ...), kind=kLoop, calls=%fused_computation.25 | loop fusion | flops 1152 | bytes 3596 | tf_op jit(solution)/shard_map/add | solution.py:87
  76.7 0.8 fusion.2
  77.5 1.0 %fusion.4 = f32[4,4,128]{2,1,0:T(4,128)S(1)} fusion(f32[4,512,128,4]{2,1,3,0:T(8,128)S(1)} %get-tuple-element.320, f32[4,4,128]{2,1,0:T(4,128)S(1)} %get-tuple-element.400, pred[128,512]{0,1:T(8,128)(4,1)S(1)} %broadcast_compare_fusion), kind=kLoop, calls=%fused_computation.5 | loop fusion | flops 5240832 | bytes 4276224 | tf_op jit(solution)/shard_map/while/body/eval_jaxpr/cond/branch_0_fun/reduce_sum | solution.py:30
  78.5 1.7 %fusion.11 = f32[128,4,4,128]{3,0,2,1:T(8,128)S(1)} fusion(f32[4,512,128,4]{2,1,3,0:T(8,128)S(1)} %get-tuple-element.320, f32[4,4,128]{2,1,0:T(4,128)S(1)} %get-tuple-element.400, pred[128,512]{0,1:T(8,128)(4,1)S(1)} %broadcast_compare_fusion, f32[128,4,4,128]{3,0,2,1:T(8,128)S(1)} %get-tuple-element.261, bf16[2,512,4,128]{3,1,2,0:T(8,128)(2,1)S(1)} %copy-done.2, ...), kind=kOutput, calls=%fused_computation.9 | convolution fusion | flops 274202624 | bytes 6897668 | tf_op jit(solution)/shard_map/while/body/eval_jaxpr/cond/branch_0_fun/kgrs,skd->rkgd/dot_general | solution.py:32
  81.0 1.2 %convert_element_type.46 = bf16[1,128,2048]{2,1,0:T(8,128)(2,1)} reshape(bf16[128,4,4,128]{3,2,1,0:T(4,128)(2,1)S(1)} %copy.24) | data formatting | bytes 1048576 | tf_op jit(solution)/shard_map/convert_element_type | solution.py:99
  (46 shorter events, 5.1 us)
Async XLA Ops:
  7.2 53.3 %copy-start = (bf16[1,128,4096]{2,1,0:T(8,128)(2,1)S(1)}, bf16[1,128,4096]{2,1,0:T(8,128)(2,1)}, u32[]{:S(2)}) copy-start(bf16[1,128,4096]{2,1,0:T(8,128)(2,1)} %param.15) | copy-start | bytes 3145732
  7.2 53.3 %copy-start.1 = (bf16[1,128,4096]{2,1,0:T(8,128)(2,1)S(1)}, bf16[1,128,4096]{2,1,0:T(8,128)(2,1)}, u32[]{:S(2)}) copy-start(bf16[1,128,4096]{2,1,0:T(8,128)(2,1)} %param.16) | copy-start | bytes 3145732
  7.2 53.3 %copy-start.3 = (f32[4096]{0:T(1024)S(1)}, f32[4096]{0:T(1024)}, u32[]{:S(2)}) copy-start(f32[4096]{0:T(1024)} %param.17) | copy-start | bytes 49156
  7.2 54.9 %all-gather.3.cloned.1.call-start = ((), (), s32[]{:S(2)}) async-start(), calls=%async_computation | async-start | bytes 1179648 | tf_op jit(solution)/shard_map/all_gather | solution.py:93
  7.9 55.6 %all-gather.5.cloned.1.call-start = ((), (), s32[]{:S(2)}) async-start(), calls=%async_computation.1 | async-start | bytes 1179648 | tf_op jit(solution)/shard_map/all_gather | solution.py:94
  69.7 1.8 %copy-start.2 = (bf16[2,512,4,128]{3,1,2,0:T(8,128)(2,1)S(1)}, bf16[2,512,4,128]{3,1,2,0:T(8,128)(2,1)}, u32[]{:S(2)}) copy-start(bf16[2,512,4,128]{3,1,2,0:T(8,128)(2,1)} %get-tuple-element.262) | copy-start | bytes 3145732 | tf_op jit(solution)/shard_map/while/body/eval_jaxpr/cond
  76.7 1.8 %copy-start.2 = (bf16[2,512,4,128]{3,1,2,0:T(8,128)(2,1)S(1)}, bf16[2,512,4,128]{3,1,2,0:T(8,128)(2,1)}, u32[]{:S(2)}) copy-start(bf16[2,512,4,128]{3,1,2,0:T(8,128)(2,1)} %get-tuple-element.262) | copy-start | bytes 3145732 | tf_op jit(solution)/shard_map/while/body/eval_jaxpr/cond
Sparse Core Ops, SparseCore 0:
  9.9 25.9 all-gather.2
  37.7 23.9 all-gather.4
where the time goes:
time: 90.1 us; the launch traced here: 89.6 us
  blocking collectives  42.3 us (47%)
  other arithmetic  15.4 us (17%)
  between operations  14.2 us (16%)
  local copies, waits for them, and re-layouts  8.61 us (10%)
  matrix products  4.87 us (5%)
  loops' own time  2.82 us (3%)
  waiting for transfers between devices  1.4 us (2%)
    psum x1, blocking collectives, norm_backward(): gain_grad = lax.psum(partial_grad, ('ctx', 'dp'))  42.3 us
    dot_general x2, matrix products, dense_update(): jnp.einsum('kgrs,skd->rkgd', probs, value_rows, preferred_element_type=jn...  3.37 us
    unnamed x10, local copies, waits for them, and re-layouts  2.88 us
    another operation x1, loops' own time, fold_piece(): lax.scan(step_fn, carry, (key_rows.reshape(steps, block, heads, HEAD_WIDT...  2.66 us
    add x2, other arithmetic, attention(): jnp.where(local < half, mine[0], mine[1]) * half + local % half  2.54 us
    reduce_sum x1, other arithmetic, norm_backward(): partial_grad = jnp.sum(grad_f * normed, axis=0)  2.36 us
    reduce_sum x2, other arithmetic, dense_update(): total = total * factor + jnp.sum(weights, axis=-1)  2.02 us
    reduce_max x1, other arithmetic, update(): later = jnp.min(k_positions) > jnp.max(q_positions)  1.93 us
  transfers between devices with their start and end apart: 2, of which 0 were waited for; matrix products, arithmetic and copies ran while one was open for 14% of the time, Pallas kernels for 0%

commit v1 on v0

--- a/solution.py
+++ b/solution.py
@@ -107,7 +107,7 @@
     inv_rms = 1.0 / jnp.sqrt(jnp.mean(resid_f * resid_f, axis=-1, keepdims=True) + 1e-05)
     normed = resid_f * inv_rms
     partial_grad = jnp.sum(grad_f * normed, axis=0)
-    gain_grad = lax.psum(partial_grad, ("ctx", "dp"))
+    gain_grad = lax.psum(lax.psum(partial_grad, "ctx"), "dp")
     scaled = gain[None, :] * grad_f
     resid_grad = (
         (scaled - normed * jnp.mean(scaled * normed, axis=-1, keepdims=True)) * inv_rms

time: 90.1 us -> 93 us (1.032)
  the two profiles are of different devices: /device:TPU:1 before, /device:TPU:0 now
where the time goes in v1:
time: 93 us; the launch traced here: 92.6 us
  blocking collectives  45.2 us (49%)
  other arithmetic  15.4 us (17%)
  between operations  14.2 us (15%)
  local copies, waits for them, and re-layouts  8.61 us (9%)
  matrix products  4.87 us (5%)
  loops' own time  2.82 us (3%)
  waiting for transfers between devices  1.4 us (2%)
    psum x2, blocking collectives, norm_backward(): gain_grad = lax.psum(lax.psum(partial_grad, 'ctx'), 'dp')  45.2 us
    dot_general x2, matrix products, dense_update(): jnp.einsum('kgrs,skd->rkgd', probs, value_rows, preferred_element_type=jn...  3.37 us
    unnamed x10, local copies, waits for them, and re-layouts  2.88 us
    another operation x1, loops' own time, fold_piece(): lax.scan(step_fn, carry, (key_rows.reshape(steps, block, heads, HEAD_WIDT...  2.66 us
    add x2, other arithmetic, attention(): jnp.where(local < half, mine[0], mine[1]) * half + local % half  2.54 us
    reduce_sum x1, other arithmetic, norm_backward(): partial_grad = jnp.sum(grad_f * normed, axis=0)  2.36 us
    reduce_sum x2, other arithmetic, dense_update(): total = total * factor + jnp.sum(weights, axis=-1)  2.02 us
    reduce_max x1, other arithmetic, update(): later = jnp.min(k_positions) > jnp.max(q_positions)  1.93 us
  transfers between devices with their start and end apart: 2, of which 0 were waited for; matrix products, arithmetic and copies ran while one was open for 14% of the time, Pallas kernels for 0%

profile of v1, /device:TPU:0, one launch (start us, length us, event | category | flops | bytes accessed | tf_op | source)
XLA Modules:
  0.0 92.6 jit_solution(5314909566116817877)
XLA Ops:
  8.7 0.7 dynamic_slice.27
  10.0 1.3 %copy.20 = bf16[1,128,2048]{1,2,0:T(8,128)(2,1)S(1)} copy(bf16[1,128,2048]{2,1,0:T(8,128)(2,1)} %param.11) | data formatting | bytes 1048576 | tf_op args[0]
  11.6 0.7 select_reduce_fusion
  12.4 1.5 %fusion.38 = f32[128]{0:T(128)S(1)} fusion(bf16[1,128,4096]{2,1,0:T(8,128)(2,1)} %param.15), kind=kLoop, calls=%fused_computation.45 | loop fusion | flops 1572736 | bytes 1049088 | tf_op jit(solution)/shard_map/reduce_sum | solution.py:107
  13.9 1.9 %fusion.47 = s32[]{:T(128)} fusion(s32[]{:T(128)} %bitcast.11, s32[]{:T(128)} %bitcast.10), kind=kLoop, calls=%fused_computation.69 | loop fusion | flops 1407 | bytes 12 | tf_op jit(solution)/shard_map/while/body/eval_jaxpr/reduce_max | solution.py:38
  15.9 2.4 %fusion.34 = (f32[4096]{0:T(1024)S(1)}, f32[128]{0:T(128)S(1)}) fusion(bf16[1,128,4096]{2,1,0:T(8,128)(2,1)} %param.15, bf16[1,128,4096]{2,1,0:T(8,128)(2,1)} %param.16, f32[128]{0:T(128)S(1)} %add_rsqrt_fusion, f32[4096]{0:T(1024)} %param.17), kind=kLoop, calls=%fused_computation.41 | loop fusion | flops 4190080 | bytes 2130944 | tf_op jit(solution)/shard_map/reduce_sum | solution.py:109
  18.2 25.6 %psum.14 = f32[4096]{0:T(1024)S(1)} all-reduce(f32[4096]{0:T(1024)S(1)} %get-tuple-element.291), channel_id=1, replica_groups=mesh['ctx'=8,'dp'=4] {'ctx'}, use_global_device_ids=true, to_apply=%region_12.13 | all-reduce | flops 4096 | bytes 32768 | tf_op jit(solution)/shard_map/psum | solution.py:110
  43.9 19.6 %psum.15 = f32[4096]{0:T(1024)} all-reduce(f32[4096]{0:T(1024)S(1)} %psum.14), channel_id=1, replica_groups=mesh['ctx'=8,'dp'=4] {'dp'}, use_global_device_ids=true, to_apply=%region_13.14 | all-reduce | flops 4096 | bytes 32768 | tf_op jit(solution)/shard_map/psum | solution.py:110
  63.5 1.5 %fusion.37 = bf16[1,128,4096]{2,1,0:T(8,128)(2,1)} fusion(bf16[1,128,4096]{2,1,0:T(8,128)(2,1)S(1)} %copy-done.1, bf16[1,128,4096]{2,1,0:T(8,128)(2,1)S(1)} %copy-done, f32[128]{0:T(128)S(1)} %broadcast_multiply_fusion.1, f32[128]{0:T(128)S(1)} %add_rsqrt_fusion, f32[4096]{0:T(1024)S(1)} %copy-done.3), kind=kLoop, calls=%fused_computation.44 | loop fusion | flops 4194304 | bytes 3163136 | tf_op jit(solution)/shard_map/convert_element_type | solution.py:114
  65.0 1.3 %reshape_reshape_squeeze.6 = bf16[2,512,4,128]{3,2,1,0:T(4,128)(2,1)S(1)} reshape(bf16[1,1024,512]{2,1,0:T(8,128)(2,1)} %all-gather.3.cloned.1.call-done) | data formatting | bytes 2097152 | tf_op jit(solution)/shard_map/reshape;reshape;squeeze | solution.py:65
  66.5 1.3 %reshape_reshape_squeeze.7 = bf16[2,512,4,128]{3,2,1,0:T(4,128)(2,1)S(1)} reshape(bf16[1,1024,512]{2,1,0:T(8,128)(2,1)} %all-gather.5.cloned.1.call-done) | data formatting | bytes 2097152 | tf_op jit(solution)/shard_map/reshape;reshape;squeeze | solution.py:66
  67.9 1.1 %copy.23 = bf16[2,512,4,128]{3,1,2,0:T(8,128)(2,1)} copy(bf16[2,512,4,128]{3,2,1,0:T(4,128)(2,1)S(1)} %reshape_reshape_squeeze.7) | data formatting | bytes 2097152
  69.1 14.0 %while.16 = (s32[]{:T(128)}, f32[4,4,128]{2,1,0:T(4,128)S(1)}, f32[4,4,128]{2,1,0:T(4,128)S(1)}, f32[128,4,4,128]{3,0,2,1:T(8,128)S(1)}, s32[2,512]{1,0:T(2,128)...) while((s32[]{:T(128)}, f32[4,4,128]{2,1,0:T(4,128)S(1)}, ...), condition=%wide.region_8.9_spmd.clone, body=%wide.region_2.8_spmd.clone.sunk | while | flops 551100160 | bytes 20852624 | solution.py:61
  71.2 5.0 %conditional.3 = ((f32[4,4,128]{2,1,0:T(4,128)S(1)}, f32[4,4,128]{2,1,0:T(4,128)S(1)}, f32[128,4,4,128]{3,0,2,1:T(8,128)S(1)})) conditional(s32[]{:T(128)} %convert_element_type.103, (s32[1,512]{1,0:T(1,128)S(1)}, s32[128]{0:T(128)S(1)}, bf16[2,512,4,128]{3,1,2,0:T(8,128)(2,1)S(1)}, s32[]{:T(128)}, bf16[128,4,4,128]{3,0,2,1:T(8,128)(2,1)S(1)}, ...), branch_computations={%region_4.6_spmd.clone, %region_7.7_spmd} | conditional | flops 551099520 | bytes 20846672 | solution.py:39
  71.2 1.3 %fusion.24 = s32[128]{0:T(128)S(1)} fusion(s32[128]{0:T(128)S(1)} %get-tuple-element.268, s32[128]{0:T(128)S(1)} %get-tuple-element.267, s32[128]{0:T(128)S(1)} %get-tuple-element.272, s32[128]{0:T(128)S(1)} %get-tuple-element.272, s32[128]{0:T(128)S(1)} %get-tuple-element.272, s32[128]{0:T(128)S(1)} %get-tuple-element.272, s32[]{:T(128)} %get-tuple-element.273, ...), kind=kLoop, calls=%fused_computation.25 | loop fusion | flops 1152 | bytes 3596 | tf_op jit(solution)/shard_map/add | solution.py:87
  72.6 0.8 fusion.2
  73.4 1.0 %fusion.4 = f32[4,4,128]{2,1,0:T(4,128)S(1)} fusion(f32[4,512,128,4]{2,1,3,0:T(8,128)S(1)} %get-tuple-element.320, f32[4,4,128]{2,1,0:T(4,128)S(1)} %get-tuple-element.400, pred[128,512]{0,1:T(8,128)(4,1)S(1)} %broadcast_compare_fusion), kind=kLoop, calls=%fused_computation.5 | loop fusion | flops 5240832 | bytes 4276224 | tf_op jit(solution)/shard_map/while/body/eval_jaxpr/cond/branch_0_fun/reduce_sum | solution.py:30
  74.4 1.7 %fusion.11 = f32[128,4,4,128]{3,0,2,1:T(8,128)S(1)} fusion(f32[4,512,128,4]{2,1,3,0:T(8,128)S(1)} %get-tuple-element.320, f32[4,4,128]{2,1,0:T(4,128)S(1)} %get-tuple-element.400, pred[128,512]{0,1:T(8,128)(4,1)S(1)} %broadcast_compare_fusion, f32[128,4,4,128]{3,0,2,1:T(8,128)S(1)} %get-tuple-element.261, bf16[2,512,4,128]{3,1,2,0:T(8,128)(2,1)S(1)} %copy-done.2, ...), kind=kOutput, calls=%fused_computation.9 | convolution fusion | flops 274202624 | bytes 6897668 | tf_op jit(solution)/shard_map/while/body/eval_jaxpr/cond/branch_0_fun/kgrs,skd->rkgd/dot_general | solution.py:32
  78.2 5.0 %conditional.3 = ((f32[4,4,128]{2,1,0:T(4,128)S(1)}, f32[4,4,128]{2,1,0:T(4,128)S(1)}, f32[128,4,4,128]{3,0,2,1:T(8,128)S(1)})) conditional(s32[]{:T(128)} %convert_element_type.103, (s32[1,512]{1,0:T(1,128)S(1)}, s32[128]{0:T(128)S(1)}, bf16[2,512,4,128]{3,1,2,0:T(8,128)(2,1)S(1)}, s32[]{:T(128)}, bf16[128,4,4,128]{3,0,2,1:T(8,128)(2,1)S(1)}, ...), branch_computations={%region_4.6_spmd.clone, %region_7.7_spmd} | conditional | flops 551099520 | bytes 20846672 | solution.py:39
  78.2 1.3 %fusion.24 = s32[128]{0:T(128)S(1)} fusion(s32[128]{0:T(128)S(1)} %get-tuple-element.268, s32[128]{0:T(128)S(1)} %get-tuple-element.267, s32[128]{0:T(128)S(1)} %get-tuple-element.272, s32[128]{0:T(128)S(1)} %get-tuple-element.272, s32[128]{0:T(128)S(1)} %get-tuple-element.272, s32[128]{0:T(128)S(1)} %get-tuple-element.272, s32[]{:T(128)} %get-tuple-element.273, ...), kind=kLoop, calls=%fused_computation.25 | loop fusion | flops 1152 | bytes 3596 | tf_op jit(solution)/shard_map/add | solution.py:87
  79.6 0.8 fusion.2
  80.4 1.0 %fusion.4 = f32[4,4,128]{2,1,0:T(4,128)S(1)} fusion(f32[4,512,128,4]{2,1,3,0:T(8,128)S(1)} %get-tuple-element.320, f32[4,4,128]{2,1,0:T(4,128)S(1)} %get-tuple-element.400, pred[128,512]{0,1:T(8,128)(4,1)S(1)} %broadcast_compare_fusion), kind=kLoop, calls=%fused_computation.5 | loop fusion | flops 5240832 | bytes 4276224 | tf_op jit(solution)/shard_map/while/body/eval_jaxpr/cond/branch_0_fun/reduce_sum | solution.py:30
  81.4 1.7 %fusion.11 = f32[128,4,4,128]{3,0,2,1:T(8,128)S(1)} fusion(f32[4,512,128,4]{2,1,3,0:T(8,128)S(1)} %get-tuple-element.320, f32[4,4,128]{2,1,0:T(4,128)S(1)} %get-tuple-element.400, pred[128,512]{0,1:T(8,128)(4,1)S(1)} %broadcast_compare_fusion, f32[128,4,4,128]{3,0,2,1:T(8,128)S(1)} %get-tuple-element.261, bf16[2,512,4,128]{3,1,2,0:T(8,128)(2,1)S(1)} %copy-done.2, ...), kind=kOutput, calls=%fused_computation.9 | convolution fusion | flops 274202624 | bytes 6897668 | tf_op jit(solution)/shard_map/while/body/eval_jaxpr/cond/branch_0_fun/kgrs,skd->rkgd/dot_general | solution.py:32
  83.9 1.2 %convert_element_type.46 = bf16[1,128,2048]{2,1,0:T(8,128)(2,1)} reshape(bf16[128,4,4,128]{3,2,1,0:T(4,128)(2,1)S(1)} %copy.24) | data formatting | bytes 1048576 | tf_op jit(solution)/shard_map/convert_element_type | solution.py:99
  (47 shorter events, 5.8 us)
Async XLA Ops:
  7.2 56.3 %copy-start = (bf16[1,128,4096]{2,1,0:T(8,128)(2,1)S(1)}, bf16[1,128,4096]{2,1,0:T(8,128)(2,1)}, u32[]{:S(2)}) copy-start(bf16[1,128,4096]{2,1,0:T(8,128)(2,1)} %param.15) | copy-start | bytes 3145732
  7.2 56.3 %copy-start.1 = (bf16[1,128,4096]{2,1,0:T(8,128)(2,1)S(1)}, bf16[1,128,4096]{2,1,0:T(8,128)(2,1)}, u32[]{:S(2)}) copy-start(bf16[1,128,4096]{2,1,0:T(8,128)(2,1)} %param.16) | copy-start | bytes 3145732
  7.2 56.3 %copy-start.3 = (f32[4096]{0:T(1024)S(1)}, f32[4096]{0:T(1024)}, u32[]{:S(2)}) copy-start(f32[4096]{0:T(1024)} %param.17) | copy-start | bytes 49156
  7.2 57.8 %all-gather.3.cloned.1.call-start = ((), (), s32[]{:S(2)}) async-start(), calls=%async_computation | async-start | bytes 1179648 | tf_op jit(solution)/shard_map/all_gather | solution.py:93
  7.9 58.6 %all-gather.5.cloned.1.call-start = ((), (), s32[]{:S(2)}) async-start(), calls=%async_computation.1 | async-start | bytes 1179648 | tf_op jit(solution)/shard_map/all_gather | solution.py:94
  72.6 1.8 %copy-start.2 = (bf16[2,512,4,128]{3,1,2,0:T(8,128)(2,1)S(1)}, bf16[2,512,4,128]{3,1,2,0:T(8,128)(2,1)}, u32[]{:S(2)}) copy-start(bf16[2,512,4,128]{3,1,2,0:T(8,128)(2,1)} %get-tuple-element.262) | copy-start | bytes 3145732 | tf_op jit(solution)/shard_map/while/body/eval_jaxpr/cond
  79.6 1.8 %copy-start.2 = (bf16[2,512,4,128]{3,1,2,0:T(8,128)(2,1)S(1)}, bf16[2,512,4,128]{3,1,2,0:T(8,128)(2,1)}, u32[]{:S(2)}) copy-start(bf16[2,512,4,128]{3,1,2,0:T(8,128)(2,1)} %get-tuple-element.262) | copy-start | bytes 3145732 | tf_op jit(solution)/shard_map/while/body/eval_jaxpr/cond
Sparse Core Ops, SparseCore 0:
  9.9 26.1 all-gather.2
  38.0 23.3 all-gather.4
